TPU v7x, 1024 devices: a whole 8x8x8 slice. The times are simulated.
1024 devices in a mesh: batch: 64 (over y_hi, x, core), seq: 16 (over z, y_lo).
Axes of the slice: x: 8, y: 8 (y_hi: 4, y_lo: 2; y = y_hi * 2 + y_lo), z: 8, core: 2. Of those that a mesh axis runs over, the one named last changes fastest.
Arguments:
- queries: bfloat16 [64, 2048, 1280], P('batch', 'seq'), may hold values from -120 to 120
- keys: bfloat16 [64, 2048, 1280], P('batch', 'seq'), may hold values from -7.5 to 7.5
- values: bfloat16 [64, 2048, 1280], P('batch', 'seq'), may hold values from -6 to 6
- residual_in: bfloat16 [64, 2048, 1280], P('batch', 'seq'), may hold values from -3 to 3
- w_out: bfloat16 [1280, 1280], replicated, may hold values from -0.15625 to 0.15625
- ln_gain: float32 [1280], replicated, may hold values from 0.5 to 1.5
- w_proj: bfloat16 [1280, 1024], replicated, may hold values from -0.15625 to 0.15625
- texts: float32 [64, 1024], P('batch', 'seq'), may hold values from -1200 to 1200
- labels: int32 [64], replicated, may hold values from 0 to 63, each once
Outputs:
- hidden_out: bfloat16 [64, 2048, 1280], P('batch', 'seq')
- image_loss: float32 [64], P('batch')
- text_loss: float32 [64], P('batch')
All inputs are finite; a program needn't handle non-finite values.
Results may differ from a plain program's by a relative error of at most 0.0034.
Values may be sent and summed in bfloat16 or wider, within the bound.
A program may use at most 32 MiB of HBM per device.

v0:
```python
import jax
import jax.numpy as jnp
from jax import lax
from jax.sharding import Mesh
from jax.sharding import PartitionSpec as P

HEADS = 16
HEAD_DIM = 80
PATCHES = 2048
SEQ = ("seq_0", "seq_1")


def cut_along(value, dim, length):
    shape = value.shape
    blocks = value.reshape(*shape[:dim], length, shape[dim] // length, *shape[dim + 1 :])
    return jnp.moveaxis(blocks, dim, 0)


def laid_out(blocks, dim):
    blocks = jnp.moveaxis(blocks, 0, dim)
    shape = blocks.shape
    return blocks.reshape(*shape[:dim], shape[dim] * shape[dim + 1], *shape[dim + 2 :])


def moved_by_axis(blocks, axes, sequence):
    inside = blocks.shape[1:]
    result = blocks.reshape(*(lax.axis_size(a) for a in axes), *inside)
    for k in sequence:
        result = lax.all_to_all(result, axes[k], k, k, tiled=True)
    return result.reshape(-1, *inside)


def stepwise_exchange(value, axes, sequence, split_dim, concat_dim):
    blocks = cut_along(value, split_dim, lax.axis_size(axes))
    return laid_out(moved_by_axis(blocks, axes, sequence), concat_dim)


def sent_and_summed(value, axis, dim):
    blocks = cut_along(value, dim, lax.axis_size(axis))
    arrived = lax.all_to_all(blocks, axis, split_axis=0, concat_axis=0, tiled=True)
    return arrived.sum(axis=0)


def in_one_piece(arrays, axis, dim, along):
    both = jnp.concatenate(arrays, axis=along)
    result, at, finished = (lax.all_gather(both, axis, axis=dim, tiled=True), 0, [])
    for a in arrays:
        finished.append(lax.slice_in_dim(result, at, at + a.shape[along], axis=along))
        at += a.shape[along]
    return tuple(finished)


def from_everyone(value, axis):
    copies = jnp.broadcast_to(value, (lax.axis_size(axis), *value.shape))
    return lax.all_to_all(copies, axis, split_axis=0, concat_axis=0, tiled=True)


def taken_together(value, axis):
    everything = from_everyone(value, axis)
    return jnp.sum(everything, axis=0)


def together(arrays, axis):
    ends = [0]
    for a in arrays:
        ends.append(ends[-1] + a.size)
    subtotal = taken_together(jnp.concatenate([a.ravel() for a in arrays]), axis)
    return tuple((subtotal[b:e].reshape(a.shape) for a, b, e in zip(arrays, ends, ends[1:])))


def row_lse(logits, axis):
    maxima = jnp.max(logits, axis=axis, keepdims=True)
    return jnp.squeeze(maxima, axis) + jnp.log(jnp.sum(jnp.exp(logits - maxima), axis=axis))


def body(queries, keys, values, residual_in, w_out, ln_gain, w_proj, texts, labels):
    seq_count = lax.axis_size(SEQ)
    images_here, tok_rows, features = queries.shape
    head_count = HEADS // seq_count
    head_cols = head_count * HEAD_DIM
    score_scale = HEAD_DIM ** (-0.5)
    query_all = lax.all_to_all(queries, SEQ, split_axis=2, concat_axis=1, tiled=True)
    key_all = lax.all_to_all(keys, SEQ, split_axis=2, concat_axis=1, tiled=True)
    value_all = lax.all_to_all(values, SEQ, split_axis=2, concat_axis=1, tiled=True)
    items = query_all.shape[0]
    length = query_all.shape[1]
    block_rows = min(512, length)
    query_heads = query_all.reshape(items, length, head_count, HEAD_DIM)
    key_heads = key_all.reshape(items, length, head_count, HEAD_DIM)
    value_heads = value_all.reshape(items, length, head_count, HEAD_DIM)

    def one_block(offset):
        query_block = lax.dynamic_slice_in_dim(query_heads, offset, block_rows, 1)
        scores = (
            jnp.einsum(
                "nqhd,nkhd->nhqk", query_block, key_heads, preferred_element_type=jnp.float32
            )
            * score_scale
        )
        maxima = jnp.max(scores, axis=-1, keepdims=True)
        weights = jnp.exp(scores - maxima)
        weights = (weights / jnp.sum(weights, axis=-1, keepdims=True)).astype(jnp.bfloat16)
        mixed = jnp.einsum(
            "nhqk,nkhd->nqhd", weights, value_heads, preferred_element_type=jnp.float32
        )
        return mixed.astype(jnp.bfloat16).reshape(items, block_rows, head_cols)

    offsets = jnp.arange(length // block_rows) * block_rows
    blocks = lax.map(one_block, offsets)
    attended = jnp.moveaxis(blocks, 0, 1).reshape(items, length, head_cols)
    attended = stepwise_exchange(attended, SEQ, (0, 1), 1, 2)
    mixed_out = jnp.dot(attended.reshape(-1, features), w_out, preferred_element_type=jnp.float32)
    summed = residual_in.astype(jnp.float32) + mixed_out.reshape(images_here, tok_rows, features)
    hidden_out = summed.astype(jnp.bfloat16)
    centred = summed - jnp.mean(summed, axis=-1, keepdims=True)
    variance = jnp.mean(centred * centred, axis=-1, keepdims=True)
    normed = centred * lax.rsqrt(variance + 1e-05) * ln_gain
    pool_part = jnp.sum(normed, axis=1) / PATCHES
    projected = jnp.dot(pool_part, w_proj.astype(jnp.float32), precision=lax.Precision.HIGHEST)
    embed_piece = sent_and_summed(projected, SEQ, 1)
    gathered, text_all = in_one_piece((embed_piece, texts), "batch", 0, 1)
    logit_part = jnp.dot(gathered, text_all.T, precision=lax.Precision.HIGHEST)
    logit_raw, squares = together((logit_part, jnp.sum(gathered * gathered, axis=1)), SEQ)
    logits = logit_raw * lax.rsqrt(squares + 1e-06)[:, None]
    matched = labels[:, None] == jnp.arange(logits.shape[1], dtype=jnp.int32)[None, :]
    picked = jnp.where(matched, logits, jnp.float32(0.0))
    image_all = row_lse(logits, 1) - jnp.sum(picked, axis=1)
    text_every = row_lse(logits, 0) - jnp.sum(picked, axis=0)
    first_row = lax.axis_index("batch") * images_here
    image_loss = lax.dynamic_slice_in_dim(image_all, first_row, images_here, 0)
    text_loss = lax.dynamic_slice_in_dim(text_every, first_row, images_here, 0)
    return (hidden_out, image_loss, text_loss)


def solution(mesh):
    split = Mesh(mesh.devices.reshape(mesh.shape["batch"], 8, 2), ("batch", "seq_0", "seq_1"))
    return jax.shard_map(
        body,
        mesh=split,
        in_specs=(
            P("batch", SEQ, None),
            P("batch", SEQ, None),
            P("batch", SEQ, None),
            P("batch", SEQ, None),
            P(),
            P(),
            P(),
            P("batch", SEQ),
            P(),
        ),
        out_specs=(P("batch", SEQ, None), P("batch"), P("batch")),
        check_vma=False,
    )
```

profile of v0, /device:TPU:1, one launch (start us, length us, event | category | flops | bytes accessed | tf_op | source)
XLA Modules:
  0.0 279.3 jit_solution(5982319509038124196)
XLA Ops:
  0.6 2.2 copy.46
  2.9 0.5 broadcast.67
  3.4 9.1 %reduce.9 = bf16[1280,128]{1,0:T(8,128)(2,1)} reduce(bf16[1280,1,128]{2,1,0:T(2,128)(2,1)} %bitcast.88, bf16[]{:T(256)} %broadcast.67), dimensions={1}, to_apply=%bitcast.63.reduce_sub_computation | reduce | bytes 655362
  12.5 1.8 reshape.131
  14.3 18.5 %all-to-all-start = ((bf16[16,2,5120]{2,1,0:T(2,128)(2,1)}), bf16[16,2,5120]{2,1,0:T(2,128)(2,1)}, u32[]{:S(2)}, u32[]{:S(2)}) async-start(bf16[16,2,5120]{2,1,0:T(2,128)(2,1)} %reshape.131), calls=%async_computation | async-start | bytes 655360 | tf_op jit(solution)/shard_map/all_to_all | solution.py:82
  32.8 2.1 copy.48
  34.9 9.1 %reduce.10 = bf16[1280,128]{1,0:T(8,128)(2,1)} reduce(bf16[1280,1,128]{2,1,0:T(2,128)(2,1)} %bitcast.90, bf16[]{:T(256)} %broadcast.67), dimensions={1}, to_apply=%bitcast.65.reduce_sub_computation | reduce | bytes 655362
  44.0 1.8 reshape.133
  45.8 7.6 %all-to-all-start.1 = ((bf16[16,2,5120]{2,1,0:T(2,128)(2,1)}), bf16[16,2,5120]{2,1,0:T(2,128)(2,1)}, u32[]{:S(2)}, u32[]{:S(2)}) async-start(bf16[16,2,5120]{2,1,0:T(2,128)(2,1)} %reshape.133), calls=%async_computation.1 | async-start | bytes 655360 | tf_op jit(solution)/shard_map/all_to_all | solution.py:83
  53.4 2.1 copy.50
  55.5 9.1 %reduce.11 = bf16[1280,128]{1,0:T(8,128)(2,1)} reduce(bf16[1280,1,128]{2,1,0:T(2,128)(2,1)} %bitcast.89, bf16[]{:T(256)} %broadcast.67), dimensions={1}, to_apply=%bitcast.67.reduce_sub_computation | reduce | bytes 655362
  64.6 1.8 reshape.135
  66.4 7.6 %all-to-all-start.2 = ((bf16[16,2,5120]{2,1,0:T(2,128)(2,1)}), bf16[16,2,5120]{2,1,0:T(2,128)(2,1)}, u32[]{:S(2)}, u32[]{:S(2)}) async-start(bf16[16,2,5120]{2,1,0:T(2,128)(2,1)} %reshape.135), calls=%async_computation.2 | async-start | bytes 655360 | tf_op jit(solution)/shard_map/all_to_all | solution.py:84
  74.0 3.2 %reshape.132 = bf16[1280,1,128]{2,1,0:T(2,128)(2,1)} reshape(bf16[16,2,5120]{2,1,0:T(2,128)(2,1)} %all-to-all-done) | data formatting | bytes 655360
  77.2 1.1 copy.59
  78.3 0.8 copy.47
  79.1 1.8 reshape.119
  81.0 3.2 %reshape.134 = bf16[1280,1,128]{2,1,0:T(2,128)(2,1)} reshape(bf16[16,2,5120]{2,1,0:T(2,128)(2,1)} %all-to-all-done.1) | data formatting | bytes 655360
  84.2 1.1 copy.60
  85.3 0.8 copy.49
  86.1 1.8 reshape.120
  88.0 3.2 %reshape.136 = bf16[1280,1,128]{2,1,0:T(2,128)(2,1)} reshape(bf16[16,2,5120]{2,1,0:T(2,128)(2,1)} %all-to-all-done.2) | data formatting | bytes 655360
  91.2 1.1 copy.61
  92.3 0.8 copy.51
  93.1 1.9 reshape.121
  95.0 28.3 %while.10 = (s32[]{:T(128)}, bf16[4,1,512,80]{2,3,1,0:T(8,128)(2,1)}, s32[4]{0:T(128)S(1)}, bf16[1,2048,1,80]{1,3,2,0:T(8,128)(2,1)}, bf16[1,2048,1,80]{1,3,2,0:...) while((s32[]{:T(128)}, bf16[4,1,512,80]{2,3,1,0:T(8,128)(2,1)}, ...), condition=%wide.region_3.4_spmd, body=%wide.region_0.3_spmd.sunk | while | flops 345021440 | bytes 14723755 | solution.py:109
  95.0 0.6 dynamic_slice.24
  97.5 2.0 multiply_reduce_fusion.7
  99.5 0.8 fusion.29
  100.3 1.7 fusion.30
  102.1 0.6 dynamic_slice.24
  104.6 2.0 multiply_reduce_fusion.7
  106.6 0.8 fusion.29
  107.4 1.7 fusion.30
  109.1 0.6 dynamic_slice.24
  111.7 2.0 multiply_reduce_fusion.7
  113.6 0.8 fusion.29
  114.5 1.7 fusion.30
  116.2 0.6 dynamic_slice.24
  118.7 2.0 multiply_reduce_fusion.7
  120.7 0.8 fusion.29
  121.5 1.7 fusion.30
  123.3 1.9 copy.52
  125.2 1.8 reshape_transpose_reshape_reshape_transpose.3
  127.0 1.2 copy.53
  128.2 16.2 %all_to_all.66 = bf16[8,2,1,128,80]{3,1,4,2,0:T(2,128)(2,1)S(1)} all-to-all(bf16[8,2,1,128,80]{3,1,4,2,0:T(2,128)(2,1)S(1)} %copy.53), channel_id=1, replica_groups=mesh['batch'=64,'seq_0'=8,'seq_1'=2] {'seq_0'}, dimensions={0} | all-to-all | bytes 655360 | tf_op jit(solution)/shard_map/all_to_all | solution.py:29
  144.5 0.9 copy.54
  145.3 4.1 %all-to-all-start.4 = ((bf16[8,2,1,128,80]{3,0,4,2,1:T(8,128)(2,1)}), bf16[8,2,1,128,80]{3,0,4,2,1:T(8,128)(2,1)}, u32[]{:S(2)}, u32[]{:S(2)}) async-start(bf16[8,2,1,128,80]{3,0,4,2,1:T(8,128)(2,1)} %copy.54), calls=%async_computation.4 | async-start | bytes 655360 | tf_op jit(solution)/shard_map/all_to_all | solution.py:29
  149.4 4.4 %copy.56 = bf16[1280,1024]{0,1:T(8,128)(2,1)} copy(bf16[1280,1024]{1,0:T(8,128)(2,1)} %param.17) | data formatting | bytes 5242880 | tf_op args[6]
  153.9 1.2 copy.55
  155.1 1.7 fusion.20
  157.1 0.9 multiply_reduce_fusion.1
  158.0 3.1 %convolution_bitcast_fusion.1 = f32[16,1,64]{2,1,0:T(1,128)S(1)} fusion(f32[1280,1,1]{0,1,2:T(1,128)S(1)} %reshape.129, bf16[16,64,1280]{2,1,0:T(8,128)(2,1)S(1)} %bitcast.87), kind=kOutput, calls=%fused_computation.17 | convolution fusion | flops 15728640 | bytes 2630656 | tf_op jit(solution)/shard_map/dot_general | solution.py:119
  161.1 11.7 %all_to_all.67 = f32[16,1,64]{2,1,0:T(1,128)S(1)} all-to-all(f32[16,1,64]{2,1,0:T(1,128)S(1)} %convolution_bitcast_fusion.1), channel_id=1, replica_groups=mesh['batch'=64,'seq_0'=8,'seq_1'=2] {'seq_0','seq_1'}, dimensions={0} | all-to-all | bytes 8192 | tf_op jit(solution)/shard_map/all_to_all | solution.py:40
  172.9 87.2 %all-gather = f32[64,1,128]{2,1,0:T(1,128)S(1)} all-gather(f32[1,1,128]{2,1,0:T(1,128)S(1)} %maximum_bitcast_fusion), channel_id=1, replica_groups=mesh['batch'=64,'seq_0'=8,'seq_1'=2] {'batch'}, dimensions={0}, use_global_device_ids=true | all-gather | bytes 33280 | tf_op jit(solution)/shard_map/all_gather | solution.py:46
  260.1 0.3 fusion.13
  260.6 0.9 broadcast_in_dim.14
  261.4 3.5 %all-to-all-start.6 = ((f32[16,1,4160]{2,1,0:T(1,128)}), f32[16,1,4160]{2,1,0:T(1,128)S(1)}, u32[]{:S(2)}, u32[]{:S(2)}) async-start(f32[16,1,4160]{2,1,0:T(1,128)} %broadcast_in_dim.14), calls=%async_computation.6 | async-start | bytes 540672 | tf_op jit(solution)/shard_map/all_to_all | solution.py:55
  265.0 10.5 %all-to-all-done.6 = f32[16,1,4160]{2,1,0:T(1,128)S(1)} async-done(((f32[16,1,4160]{2,1,0:T(1,128)}), f32[16,1,4160]{2,1,0:T(1,128)S(1)}, u32[]{:S(2)}, u32[]{:S(2)}) %all-to-all-start.6) | async-done | bytes 266272 | tf_op jit(solution)/shard_map/all_to_all | solution.py:55
  275.5 0.8 reduce_sum.107
  276.3 0.7 slice.26
  277.0 0.7 fusion.19
  278.1 0.6 dynamic_slice.14
  278.7 0.6 dynamic_slice.13
  (38 shorter events, 1.1 us)
Async XLA Ops:
  0.6 154.4 %copy-start = (bf16[1280,1280]{1,0:T(8,128)(2,1)S(1)}, bf16[1280,1280]{1,0:T(8,128)(2,1)}, u32[]{:S(2)}) copy-start(bf16[1280,1280]{1,0:T(8,128)(2,1)} %param.15) | copy-start | bytes 9830404
  14.3 31.5 %all-to-all-start = ((bf16[16,2,5120]{2,1,0:T(2,128)(2,1)}), bf16[16,2,5120]{2,1,0:T(2,128)(2,1)}, u32[]{:S(2)}, u32[]{:S(2)}) async-start(bf16[16,2,5120]{2,1,0:T(2,128)(2,1)} %reshape.131), calls=%async_computation | async-start | bytes 655360 | tf_op jit(solution)/shard_map/all_to_all | solution.py:82
  45.8 20.6 %all-to-all-start.1 = ((bf16[16,2,5120]{2,1,0:T(2,128)(2,1)}), bf16[16,2,5120]{2,1,0:T(2,128)(2,1)}, u32[]{:S(2)}, u32[]{:S(2)}) async-start(bf16[16,2,5120]{2,1,0:T(2,128)(2,1)} %reshape.133), calls=%async_computation.1 | async-start | bytes 655360 | tf_op jit(solution)/shard_map/all_to_all | solution.py:83
  66.4 21.6 %all-to-all-start.2 = ((bf16[16,2,5120]{2,1,0:T(2,128)(2,1)}), bf16[16,2,5120]{2,1,0:T(2,128)(2,1)}, u32[]{:S(2)}, u32[]{:S(2)}) async-start(bf16[16,2,5120]{2,1,0:T(2,128)(2,1)} %reshape.135), calls=%async_computation.2 | async-start | bytes 655360 | tf_op jit(solution)/shard_map/all_to_all | solution.py:84
  97.5 2.8 %copy-start.2 = (bf16[1,2048,1,80]{1,3,2,0:T(8,128)(2,1)S(1)}, bf16[1,2048,1,80]{1,3,2,0:T(8,128)(2,1)}, u32[]{:S(2)}) copy-start(bf16[1,2048,1,80]{1,3,2,0:T(8,128)(2,1)} %get-tuple-element.128) | copy-start | bytes 983044 | tf_op jit(solution)/shard_map/while
  104.6 2.8 %copy-start.2 = (bf16[1,2048,1,80]{1,3,2,0:T(8,128)(2,1)S(1)}, bf16[1,2048,1,80]{1,3,2,0:T(8,128)(2,1)}, u32[]{:S(2)}) copy-start(bf16[1,2048,1,80]{1,3,2,0:T(8,128)(2,1)} %get-tuple-element.128) | copy-start | bytes 983044 | tf_op jit(solution)/shard_map/while
  111.7 2.8 %copy-start.2 = (bf16[1,2048,1,80]{1,3,2,0:T(8,128)(2,1)S(1)}, bf16[1,2048,1,80]{1,3,2,0:T(8,128)(2,1)}, u32[]{:S(2)}) copy-start(bf16[1,2048,1,80]{1,3,2,0:T(8,128)(2,1)} %get-tuple-element.128) | copy-start | bytes 983044 | tf_op jit(solution)/shard_map/while
  118.7 2.8 copy-start.2
  145.3 8.6 %all-to-all-start.4 = ((bf16[8,2,1,128,80]{3,0,4,2,1:T(8,128)(2,1)}), bf16[8,2,1,128,80]{3,0,4,2,1:T(8,128)(2,1)}, u32[]{:S(2)}, u32[]{:S(2)}) async-start(bf16[8,2,1,128,80]{3,0,4,2,1:T(8,128)(2,1)} %copy.54), calls=%async_computation.4 | async-start | bytes 655360 | tf_op jit(solution)/shard_map/all_to_all | solution.py:29
  153.8 3.2 %copy-start.3 = (f32[1280]{0:T(1024)S(1)}, f32[1280]{0:T(1024)}, u32[]{:S(2)}) copy-start(f32[1280]{0:T(1024)} %param.16) | copy-start | bytes 15364
  153.9 4.1 %copy-start.1 = (bf16[1280,1024]{0,1:T(8,128)(2,1)S(1)}, bf16[1280,1024]{0,1:T(8,128)(2,1)}, u32[]{:S(2)}) copy-start(bf16[1280,1024]{0,1:T(8,128)(2,1)} %copy.56) | copy-start | bytes 7864324
  155.1 17.7 %copy-start.5 = (f32[1,64]{1,0:T(1,128)S(1)}, f32[1,64]{1,0:T(1,128)}, u32[]{:S(2)}) copy-start(f32[1,64]{1,0:T(1,128)} %param.18) | copy-start | bytes 772
  155.1 122.8 %copy-start.4 = (s32[64]{0:T(128)S(1)}, s32[64]{0:T(128)}, u32[]{:S(2)}) copy-start(s32[64]{0:T(128)} %param.19) | copy-start | bytes 772
  261.4 14.1 %all-to-all-start.6 = ((f32[16,1,4160]{2,1,0:T(1,128)}), f32[16,1,4160]{2,1,0:T(1,128)S(1)}, u32[]{:S(2)}, u32[]{:S(2)}) async-start(f32[16,1,4160]{2,1,0:T(1,128)} %broadcast_in_dim.14), calls=%async_computation.6 | async-start | bytes 540672 | tf_op jit(solution)/shard_map/all_to_all | solution.py:55
where the time goes:
time: 281 us; the launch traced here: 279 us
  blocking collectives  115 us (41%)
  local copies, waits for them, and re-layouts  49.9 us (18%)
  starting transfers between devices  41.3 us (15%)
  other arithmetic  33.9 us (12%)
  matrix products  19.9 us (7%)
  waiting for transfers between devices  10.6 us (4%)
  loops' own time  7.83 us (3%)
    all_gather x1, blocking collectives, in_one_piece(): lax.all_gather(both, axis, axis=dim, tiled=True)  87.2 us
    unnamed x24, local copies, waits for them, and re-layouts  29.8 us
    unnamed x4, other arithmetic  27.5 us
    all_to_all x1, starting transfers between devices, body(): lax.all_to_all(queries, SEQ, split_axis=2, concat_axis=1, tiled=True)  18.5 us
    all_to_all x1, blocking collectives, moved_by_axis(): result = lax.all_to_all(result, axes[k], k, k, tiled=True)  16.2 us
    all_to_all x1, blocking collectives, sent_and_summed(): lax.all_to_all(blocks, axis, split_axis=0, concat_axis=0, tiled=True)  11.7 us
    all_to_all x1, waiting for transfers between devices, from_everyone(): return lax.all_to_all(copies, axis, split_axis=0, concat_axis=0, tiled=True)  10.5 us
    dot_general x4, matrix products, one_block(): jnp.einsum('nqhd,nkhd->nhqk', query_block, key_heads, preferred_element_t...  7.84 us
  transfers between devices with their start and end apart: 5, of which 2 were waited for; matrix products, arithmetic and copies ran while one was open for 16% of the time, Pallas kernels for 0%

commit v1 on v0

v1 whole, which is shorter than its diff:
```python
import math

import jax
import jax.numpy as jnp
from jax import lax
from jax.experimental import pallas as pl
from jax.experimental.pallas import tpu as pltpu
from jax.sharding import PartitionSpec as P

HEADS = 16
HD = 80
D = 1280
EMBED = 1024
PATCHES = 2048
ROWS = 128
NSEQ = 16
NZ = 8
NB = 64
NB1 = 16
NB2 = 4
CHUNK = 2 * ROWS
KB = 256
MESH = pl.DeviceIdType.MESH
F32 = jnp.float32
BF16 = jnp.bfloat16


def depth_step(t):
    half = (t + 1) // 2
    return lax.rem(4 + half * (1 - 2 * lax.rem(t, 2)) + NZ, NZ)


def kernel(
    q_hbm, k_hbm, v_hbm, res_hbm, wout_hbm, gain_ref, wproj_hbm, texts_ref, labels_ref,
    hid_hbm, img_ref, txt_ref,
    q_in, k_in, v_in, res_in, wout, wproj, hid,
    kv_send, q_send, kv_recv, q_recv, o_send, o_recv,
    k_all, vt_all, s_all, acc, t0, tex, e_buf, rows,
    load_sem, kv_ss, kv_rs, q_ss, q_rs, o_ss, o_rs, t0_ss, t0_rs, t1_ss, t1_rs, t2_ss, t2_rs,
    e_ss, e_rs, b1_ss, b1_rs, b2_ss, b2_rs,
):
    b = lax.axis_index("batch")
    s = lax.axis_index("seq")
    z, y = s // 2, lax.rem(s, 2)
    b_hi, b_lo = b // NB1, lax.rem(b, NB1)

    loads = [
        pltpu.make_async_copy(src, dst, load_sem.at[i])
        for i, (src, dst) in enumerate(
            [(k_hbm, k_in), (v_hbm, v_in), (q_hbm, q_in), (res_hbm, res_in), (wout_hbm, wout), (wproj_hbm, wproj)]
        )
    ]
    for load in loads[:4]:
        load.start()

    barrier = pltpu.get_barrier_semaphore()

    def greet_seq(r, c):
        pl.semaphore_signal(barrier, inc=1, device_id=(b, lax.rem(s + r, NSEQ)), device_id_type=MESH)
        pl.semaphore_signal(
            barrier, inc=1, device_id=(b_hi * NB1 + lax.rem(b_lo + r, NB1), s), device_id_type=MESH
        )
        return c

    lax.fori_loop(1, NSEQ, greet_seq, 0)

    def greet_far(r, c):
        pl.semaphore_signal(barrier, inc=1, device_id=(lax.rem(b + r * NB1, NB), s), device_id_type=MESH)
        return c

    lax.fori_loop(1, NB2, greet_far, 0)

    def turn(src, put):
        for c in range(D // 128):
            block = src[:, c * 128 : (c + 1) * 128].T
            i = 0
            while i < 8:
                g = c * 8 + i
                n = min(8 - i, 5 - g % 5)
                put(g // 5, (g % 5) * 16, block[i * 16 : (i + n) * 16], n * 16)
                i += n

    def put_k(h, r, value, n):
        kv_send[h, r : r + n, :] = value

    def put_v(h, r, value, n):
        kv_send[h, HD + r : HD + r + n, :] = value

    def put_q(h, r, value, n):
        q_send[h, r : r + n, :] = value

    loads[0].wait()
    turn(k_in, put_k)
    loads[1].wait()
    turn(v_in, put_v)
    loads[4].start()
    loads[5].start()

    piece = texts_ref[...]
    blank = jnp.zeros((1, 64), F32)
    even = jnp.concatenate([piece, blank], axis=1)
    odd = jnp.concatenate([blank, piece], axis=1)
    t0[s] = jnp.where(y == 0, even, odd)

    pl.semaphore_wait(barrier, 2 * (NSEQ - 1) + NB2 - 1)

    def kv_copy(to, frm):
        return pltpu.make_async_remote_copy(
            src_ref=kv_send.at[to], dst_ref=kv_recv.at[frm], send_sem=kv_ss.at[to], recv_sem=kv_rs.at[frm],
            device_id=(b, to), device_id_type=MESH,
        )

    def q_copy(to, frm):
        return pltpu.make_async_remote_copy(
            src_ref=q_send.at[to], dst_ref=q_recv.at[frm], send_sem=q_ss.at[to], recv_sem=q_rs.at[frm],
            device_id=(b, to), device_id_type=MESH,
        )

    def o_copy(to, frm):
        return pltpu.make_async_remote_copy(
            src_ref=o_send.at[to], dst_ref=o_recv.at[frm], send_sem=o_ss.at[to], recv_sem=o_rs.at[frm],
            device_id=(b, to), device_id_type=MESH,
        )

    def t0_copy(to, frm):
        return pltpu.make_async_remote_copy(
            src_ref=t0.at[frm], dst_ref=t0.at[frm], send_sem=t0_ss.at[to], recv_sem=t0_rs.at[frm],
            device_id=(b, to), device_id_type=MESH,
        )

    def e_copy(to, frm):
        return pltpu.make_async_remote_copy(
            src_ref=e_buf.at[frm], dst_ref=e_buf.at[frm], send_sem=e_ss.at[to], recv_sem=e_rs.at[frm],
            device_id=(b, to), device_id_type=MESH,
        )

    def t1_copy(to, frm):
        at = b_hi * NB1 + frm
        return pltpu.make_async_remote_copy(
            src_ref=tex.at[at], dst_ref=tex.at[at], send_sem=t1_ss.at[to], recv_sem=t1_rs.at[frm],
            device_id=(b_hi * NB1 + to, s), device_id_type=MESH,
        )

    def b1_copy(to, frm):
        at = b_hi * NB1 + frm
        return pltpu.make_async_remote_copy(
            src_ref=rows.at[at], dst_ref=rows.at[at], send_sem=b1_ss.at[to], recv_sem=b1_rs.at[frm],
            device_id=(b_hi * NB1 + to, s), device_id_type=MESH,
        )

    def t2_copy(to, frm):
        at = pl.ds(frm * NB1, NB1)
        return pltpu.make_async_remote_copy(
            src_ref=tex.at[at], dst_ref=tex.at[at], send_sem=t2_ss.at[to], recv_sem=t2_rs.at[frm],
            device_id=(to * NB1 + b_lo, s), device_id_type=MESH,
        )

    def b2_copy(to, frm):
        at = pl.ds(frm * NB1, NB1)
        return pltpu.make_async_remote_copy(
            src_ref=rows.at[at], dst_ref=rows.at[at], send_sem=b2_ss.at[to], recv_sem=b2_rs.at[frm],
            device_id=(to * NB1 + b_lo, s), device_id_type=MESH,
        )

    def others(count, me, act):
        def step(r, c):
            act(lax.rem(me + r, count))
            return c

        lax.fori_loop(1, count, step, 0)

    def by_depth(sign, act):
        def step(t, c):
            there = lax.rem(z + sign * depth_step(t) + NZ, NZ)
            for w in range(2):
                peer = 2 * there + lax.rem(y + w, 2)

                @pl.when(peer != s)
                def _():
                    act(peer)

            return c

        lax.fori_loop(0, NZ, step, 0)

    by_depth(1, lambda p: kv_copy(p, s).start())
    others(NSEQ, s, lambda p: t0_copy(p, s).start())

    loads[2].wait()
    turn(q_in, put_q)
    by_depth(1, lambda p: q_copy(p, s).start())

    others(NSEQ, s, lambda p: t0_copy(s, p).wait_recv())
    for k in range(8):
        tex[b, k : k + 1, :] = t0[2 * k] + t0[2 * k + 1]
    others(NB1, b_lo, lambda p: t1_copy(p, b_lo).start())

    kv_recv[s] = kv_send[s]
    q_recv[s] = q_send[s]
    top = lax.broadcasted_iota(jnp.int32, (16, PATCHES), 0)
    vt_all[HD : HD + 16, :] = jnp.where(top == 0, 1.0, 0.0).astype(BF16)

    others(NB1, b_lo, lambda p: t1_copy(b_lo, p).wait_recv())
    others(NB2, b_hi, lambda p: t2_copy(p, b_hi).start())

    def take_kv(t, c):
        there = lax.rem(z - depth_step(t) + NZ, NZ)
        for w in range(2):
            peer = 2 * there + w

            @pl.when(peer != s)
            def _():
                kv_copy(s, peer).wait_recv()

            block = kv_recv[peer]
            k_all[pl.ds(pl.multiple_of((2 * t + w) * ROWS, ROWS), ROWS), :] = block[:HD].T
            vt_all[0:HD, pl.ds(pl.multiple_of((2 * t + w) * ROWS, ROWS), ROWS)] = block[HD:]
        return c

    lax.fori_loop(0, NZ, take_kv, 0)

    loads[3].wait()
    factor = HD ** (-0.5) * math.log2(math.e)

    def attend(t, c):
        there = lax.rem(z - depth_step(t) + NZ, NZ)
        for w in range(2):
            peer = 2 * there + w

            @pl.when(peer != s)
            def _():
                q_copy(s, peer).wait_recv()

        qt = jnp.concatenate([q_recv[2 * there], q_recv[2 * there + 1]], axis=1)
        top8 = None
        for i in range(PATCHES // KB):
            part = jnp.dot(k_all[i * KB : (i + 1) * KB, :], qt, preferred_element_type=F32)
            s_all[i * KB : (i + 1) * KB, :] = part
            high = jnp.max(part.reshape(KB // 8, 8, CHUNK), axis=0)
            top8 = high if top8 is None else jnp.maximum(top8, high)
        maxima = jnp.max(top8, axis=0, keepdims=True)
        total = None
        for i in range(PATCHES // KB):
            weights = jnp.exp2((s_all[i * KB : (i + 1) * KB, :] - maxima) * factor).astype(BF16)
            part = jnp.dot(vt_all[:, i * KB : (i + 1) * KB], weights, preferred_element_type=F32)
            total = part if total is None else total + part
        mixed = (total[:HD] / total[HD : HD + 1]).astype(BF16)
        for w in range(2):
            peer = 2 * there + w
            value = mixed[:, w * ROWS : (w + 1) * ROWS]

            @pl.when(peer != s)
            def _():
                o_send[peer] = value
                o_copy(peer, s).start()

            @pl.when(peer == s)
            def _():
                o_recv[s] = value

        return c

    lax.fori_loop(0, NZ, attend, 0)

    others(NSEQ, s, lambda p: kv_copy(p, s).wait_send())
    others(NSEQ, s, lambda p: q_copy(p, s).wait_send())
    others(NSEQ, s, lambda p: t0_copy(p, s).wait_send())
    others(NB1, b_lo, lambda p: t1_copy(p, b_lo).wait_send())
    others(NB2, b_hi, lambda p: t2_copy(p, b_hi).wait_send())
    others(NB2, b_hi, lambda p: t2_copy(b_hi, p).wait_recv())

    acc[...] = res_in[...].astype(F32)
    loads[4].wait()

    def project(t, c):
        there = lax.rem(z + depth_step(t) + NZ, NZ)
        for w in range(2):
            peer = 2 * there + w

            @pl.when(peer != s)
            def _():
                o_copy(s, peer).wait_recv()

        part = jnp.concatenate([o_recv[2 * there], o_recv[2 * there + 1]], axis=0).T
        weight = wout[pl.ds(pl.multiple_of(there * 2 * HD, 2 * HD), 2 * HD), :]
        acc[...] += jnp.dot(part, weight, preferred_element_type=F32)
        return c

    lax.fori_loop(0, NZ, project, 0)

    pool = None
    for i in range(ROWS // 16):
        x = acc[i * 16 : (i + 1) * 16, :]
        hid[i * 16 : (i + 1) * 16, :] = x.astype(BF16)
        centred = x - jnp.sum(x, axis=1, keepdims=True) * (1.0 / D)
        variance = jnp.sum(centred * centred, axis=1, keepdims=True) * (1.0 / D)
        normed = (centred * lax.rsqrt(variance + 1e-05)).reshape(2, 8, D)
        part = normed[0] + normed[1]
        pool = part if pool is None else pool + part
    hid_copy = pltpu.make_async_copy(hid, hid_hbm.at[0], load_sem.at[6])
    hid_copy.start()

    pooled = jnp.sum(pool, axis=0, keepdims=True) * gain_ref[...] * (1.0 / PATCHES)
    first = pooled.astype(BF16).astype(F32)
    rest = pooled - first
    second = rest.astype(BF16).astype(F32)
    third = rest - second
    at = lax.broadcasted_iota(jnp.int32, (16, D), 0)
    split = jnp.where(at == 0, first, jnp.where(at == 1, second, jnp.where(at == 2, third, 0.0))).astype(BF16)
    loads[5].wait()
    projected = jnp.sum(jnp.dot(split, wproj[...], preferred_element_type=F32)[0:8], axis=0, keepdims=True)
    for k in range(8):
        e_buf[s, k : k + 1, :] = projected[:, k * 128 : (k + 1) * 128]
    others(NSEQ, s, lambda p: e_copy(p, s).start())

    others(NSEQ, s, lambda p: o_copy(p, s).wait_send())
    label_row = labels_ref[...]
    lane64 = lax.broadcasted_iota(jnp.int32, (1, 64), 1)
    own_label = jnp.sum(jnp.where(lane64 == b, label_row, 0), axis=1, keepdims=True)
    grid_i = lax.broadcasted_iota(jnp.int32, (64, 64), 0)
    grid_j = lax.broadcasted_iota(jnp.int32, (64, 64), 1)
    label_col = jnp.sum(
        jnp.where(grid_i == grid_j, jnp.broadcast_to(label_row, (64, 64)), 0), axis=1, keepdims=True
    )

    others(NSEQ, s, lambda p: e_copy(s, p).wait_recv())
    embedding = jnp.sum(e_buf[...], axis=0)
    squares = jnp.sum(jnp.sum(embedding * embedding, axis=0, keepdims=True), axis=1, keepdims=True)
    products = jnp.sum(tex[...] * embedding[None], axis=1)
    raw = jnp.sum(products.T, axis=0, keepdims=True)
    logits = raw * lax.rsqrt(squares + 1e-06)
    rows[b] = jnp.concatenate([logits, jnp.zeros((1, 64), F32)], axis=1)
    others(NB1, b_lo, lambda p: b1_copy(p, b_lo).start())

    peak = jnp.max(logits, axis=1, keepdims=True)
    lse = peak + jnp.log(jnp.sum(jnp.exp(logits - peak), axis=1, keepdims=True))
    chosen = jnp.sum(jnp.where(lane64 == own_label, logits, 0.0), axis=1, keepdims=True)
    img_ref[0] = (lse - chosen)[0, 0]
    others(NSEQ, s, lambda p: e_copy(p, s).wait_send())

    others(NB1, b_lo, lambda p: b1_copy(b_lo, p).wait_recv())
    others(NB2, b_hi, lambda p: b2_copy(p, b_hi).start())
    others(NB1, b_lo, lambda p: b1_copy(p, b_lo).wait_send())
    hid_copy.wait()
    others(NB2, b_hi, lambda p: b2_copy(b_hi, p).wait_recv())

    lane128 = lax.broadcasted_iota(jnp.int32, (64, 128), 1)
    column = jnp.sum(jnp.where(lane128 == b, rows[...].reshape(64, 128), 0.0), axis=1, keepdims=True)
    high = jnp.max(column, axis=0, keepdims=True)
    total = high + jnp.log(jnp.sum(jnp.exp(column - high), axis=0, keepdims=True))
    match = jnp.sum(jnp.where(label_col == b, column, 0.0), axis=0, keepdims=True)
    txt_ref[0] = (total - match)[0, 0]
    others(NB2, b_hi, lambda p: b2_copy(p, b_hi).wait_send())


def body(queries, keys, values, residual_in, w_out, ln_gain, w_proj, texts, labels):
    any_space = pl.BlockSpec(memory_space=pl.ANY)
    vmem = pl.BlockSpec(memory_space=pltpu.VMEM)
    smem = pl.BlockSpec(memory_space=pltpu.SMEM)
    dma = pltpu.SemaphoreType.DMA
    out = pl.pallas_call(
        kernel,
        out_shape=(
            jax.ShapeDtypeStruct((1, ROWS, D), BF16),
            jax.ShapeDtypeStruct((1,), F32),
            jax.ShapeDtypeStruct((1,), F32),
        ),
        in_specs=[any_space] * 5 + [vmem, any_space, vmem, vmem],
        out_specs=(any_space, smem, smem),
        scratch_shapes=[
            pltpu.VMEM((ROWS, D), BF16),
            pltpu.VMEM((ROWS, D), BF16),
            pltpu.VMEM((ROWS, D), BF16),
            pltpu.VMEM((ROWS, D), BF16),
            pltpu.VMEM((D, D), BF16),
            pltpu.VMEM((D, EMBED), BF16),
            pltpu.VMEM((ROWS, D), BF16),
            pltpu.VMEM((NSEQ, 2 * HD, ROWS), BF16),
            pltpu.VMEM((NSEQ, HD, ROWS), BF16),
            pltpu.VMEM((NSEQ, 2 * HD, ROWS), BF16),
            pltpu.VMEM((NSEQ, HD, ROWS), BF16),
            pltpu.VMEM((NSEQ, HD, ROWS), BF16),
            pltpu.VMEM((NSEQ, HD, ROWS), BF16),
            pltpu.VMEM((PATCHES, HD), BF16),
            pltpu.VMEM((HD + 16, PATCHES), BF16),
            pltpu.VMEM((PATCHES, CHUNK), F32),
            pltpu.VMEM((ROWS, D), F32),
            pltpu.VMEM((NSEQ, 1, 128), F32),
            pltpu.VMEM((NB, 8, 128), F32),
            pltpu.VMEM((NSEQ, 8, 128), F32),
            pltpu.VMEM((NB, 1, 128), F32),
            dma((8,)),
            dma((NSEQ,)), dma((NSEQ,)),
            dma((NSEQ,)), dma((NSEQ,)),
            dma((NSEQ,)), dma((NSEQ,)),
            dma((NSEQ,)), dma((NSEQ,)),
            dma((NB1,)), dma((NB1,)),
            dma((NB2,)), dma((NB2,)),
            dma((NSEQ,)), dma((NSEQ,)),
            dma((NB1,)), dma((NB1,)),
            dma((NB2,)), dma((NB2,)),
        ],
        compiler_params=pltpu.CompilerParams(
            collective_id=0, has_side_effects=True, vmem_limit_bytes=48 * 1024 * 1024
        ),
        name="attend_and_score",
    )(
        queries.reshape(ROWS, D),
        keys.reshape(ROWS, D),
        values.reshape(ROWS, D),
        residual_in.reshape(ROWS, D),
        w_out,
        ln_gain.reshape(1, D),
        w_proj,
        texts,
        labels.reshape(1, NB),
    )
    return out


def solution(mesh):
    return jax.shard_map(
        body,
        mesh=mesh,
        in_specs=(
            P("batch", "seq", None),
            P("batch", "seq", None),
            P("batch", "seq", None),
            P("batch", "seq", None),
            P(),
            P(),
            P(),
            P("batch", "seq"),
            P(),
        ),
        out_specs=(P("batch", "seq", None), P("batch"), P("batch")),
        check_vma=False,
    )
```

time: 281 us -> 97.2 us (0.35)
  blocking collectives: 115 us -> 0 us
  Pallas kernels: 0 us -> 84.3 us
  local copies, waits for them, and re-layouts: 49.9 us -> 8.37 us
  starting transfers between devices: 41.3 us -> 0 us
  other arithmetic: 33.9 us -> 0 us
  matrix products: 19.9 us -> 0 us
  waiting for transfers between devices: 10.6 us -> 0 us
  loops' own time: 7.83 us -> 0 us
  between operations: 0.81 us -> 4.14 us
    all_gather x1 -> x0, blocking collectives: 87.2 us -> none  [in_one_piece(): lax.all_gather(both, axis, axis=dim, tiled=True)]
    pallas_call x0 -> x1, Pallas kernels: none -> 84.3 us  [body(): pl.pallas_call(kernel, out_shape=(jax.ShapeDtypeStruct((1, ROWS, D), BF16...]
    all_to_all x5 -> x0, starting transfers between devices: 41.3 us -> none  [the longest x1 18.5 us: body(): lax.all_to_all(queries, SEQ, split_axis=2, concat_axis=1, tiled=True)]
    all_to_all x2 -> x0, blocking collectives: 27.9 us -> none  [the longest x1 16.2 us: moved_by_axis(): result = lax.all_to_all(result, axes[k], k, k, tiled=True)]
    unnamed x4 -> x0, other arithmetic: 27.5 us -> none
    unnamed x24 -> x15, local copies, waits for them, and re-layouts: 29.8 us -> 7.66 us
    dot_general x11 -> x0, matrix products: 19.9 us -> none  [the longest x4 7.84 us: one_block(): jnp.einsum('nqhd,nkhd->nhqk', query_block, key_heads, preferred_element_t...]
    all_to_all x5 -> x0, waiting for transfers between devices: 10.6 us -> none  [the longest x1 10.5 us: from_everyone(): return lax.all_to_all(copies, axis, split_axis=0, concat_axis=0, tiled=True)]
  transfers between devices with their start and end apart: 5 -> 0, of which waited for: 2 -> 0; matrix products, arithmetic and copies ran while one was open for 16% -> 0% of each run, Pallas kernels for 0% -> 0%
where the time goes in v1:
time: 97.2 us; the launch traced here: 96.8 us
  Pallas kernels  84.3 us (87%)
  local copies, waits for them, and re-layouts  8.37 us (9%)
  between operations  4.14 us (4%)
    pallas_call x1, Pallas kernels, body(): pl.pallas_call(kernel, out_shape=(jax.ShapeDtypeStruct((1, ROWS, D), BF16...  84.3 us
    unnamed x15, local copies, waits for them, and re-layouts  7.66 us

profile of v1, /device:TPU:1, one launch (start us, length us, event | category | flops | bytes accessed | tf_op | source)
XLA Modules:
  0.0 96.8 jit_solution(9970991615130521995)
XLA Ops:
  0.6 0.7 reshape.28.gain_ref
  1.3 0.0 copy-start
  1.3 1.7 %copy-done = bf16[1280,1024]{1,0:T(8,128)(2,1)S(1)} copy-done((bf16[1280,1024]{1,0:T(8,128)(2,1)S(1)}, bf16[1280,1024]{1,0:T(8,128)(2,1)}, u32[]{:S(2)}) %copy-start) | copy-done | bytes 2621464
  3.1 0.0 copy-start.1
  3.1 1.0 %copy-done.1 = bf16[1,128,1280]{2,1,0:T(8,128)(2,1)S(1)} copy-done((bf16[1,128,1280]{2,1,0:T(8,128)(2,1)S(1)}, bf16[1,128,1280]{2,1,0:T(8,128)(2,1)}, u32[]{:S(2)}) %copy-start.1) | copy-done | bytes 327704
  4.0 0.0 copy-start.2
  4.0 1.0 %copy-done.2 = bf16[1,128,1280]{2,1,0:T(8,128)(2,1)S(1)} copy-done((bf16[1,128,1280]{2,1,0:T(8,128)(2,1)S(1)}, bf16[1,128,1280]{2,1,0:T(8,128)(2,1)}, u32[]{:S(2)}) %copy-start.2) | copy-done | bytes 327704
  5.0 0.0 copy-start.3
  5.0 1.0 %copy-done.3 = bf16[1,128,1280]{2,1,0:T(8,128)(2,1)S(1)} copy-done((bf16[1,128,1280]{2,1,0:T(8,128)(2,1)S(1)}, bf16[1,128,1280]{2,1,0:T(8,128)(2,1)}, u32[]{:S(2)}) %copy-start.3) | copy-done | bytes 327704
  6.0 0.0 copy-start.4
  6.0 1.0 %copy-done.4 = bf16[1,128,1280]{2,1,0:T(8,128)(2,1)S(1)} copy-done((bf16[1,128,1280]{2,1,0:T(8,128)(2,1)S(1)}, bf16[1,128,1280]{2,1,0:T(8,128)(2,1)}, u32[]{:S(2)}) %copy-start.4) | copy-done | bytes 327704
  7.0 0.0 copy-start.5
  7.0 0.7 copy-done.5
  7.6 0.0 copy-start.6
  7.6 0.7 copy-done.6
  8.3 84.3 %attend_and_score.1 = (bf16[1,128,1280]{2,1,0:T(8,128)(2,1)S(1)}, f32[1]{0:T(128)}, f32[1]{0:T(128)}) custom-call(bf16[128,1280]{1,0:T(8,128)(2,1)S(1)} %bitcast.5, bf16[128,1280]{1,0:T(8,128)(2,1)S(1)} %bitcast.6, bf16[128,1280]{1,0:T(8,128)(2,1)S(1)} %bitcast.7, bf16[128,1280]{1,0:T(8,128)(2,1)S(1)} %bitcast.8, bf16[1280,1280]{1,0:T(8,128)(2,1)} %wout_hbm.1, ...), custom_call_target="tpu_custom_call" | custom-call | tf_op jit(solution)/shard_map/attend_and_score/pallas_call | solution.py:361
  92.5 0.7 copy.15
Async XLA Ops:
  1.3 1.7 %copy-start = (bf16[1280,1024]{1,0:T(8,128)(2,1)S(1)}, bf16[1280,1024]{1,0:T(8,128)(2,1)}, u32[]{:S(2)}) copy-start(bf16[1280,1024]{1,0:T(8,128)(2,1)} %wproj_hbm.1) | copy-start | bytes 7864324
  3.1 1.0 %copy-start.1 = (bf16[1,128,1280]{2,1,0:T(8,128)(2,1)S(1)}, bf16[1,128,1280]{2,1,0:T(8,128)(2,1)}, u32[]{:S(2)}) copy-start(bf16[1,128,1280]{2,1,0:T(8,128)(2,1)} %param.9) | copy-start | bytes 983044
  4.0 1.0 %copy-start.2 = (bf16[1,128,1280]{2,1,0:T(8,128)(2,1)S(1)}, bf16[1,128,1280]{2,1,0:T(8,128)(2,1)}, u32[]{:S(2)}) copy-start(bf16[1,128,1280]{2,1,0:T(8,128)(2,1)} %param.10) | copy-start | bytes 983044
  5.0 1.0 %copy-start.3 = (bf16[1,128,1280]{2,1,0:T(8,128)(2,1)S(1)}, bf16[1,128,1280]{2,1,0:T(8,128)(2,1)}, u32[]{:S(2)}) copy-start(bf16[1,128,1280]{2,1,0:T(8,128)(2,1)} %param.11) | copy-start | bytes 983044
  6.0 1.0 %copy-start.4 = (bf16[1,128,1280]{2,1,0:T(8,128)(2,1)S(1)}, bf16[1,128,1280]{2,1,0:T(8,128)(2,1)}, u32[]{:S(2)}) copy-start(bf16[1,128,1280]{2,1,0:T(8,128)(2,1)} %param.12) | copy-start | bytes 983044
  7.0 0.7 copy-start.5
  7.6 0.7 copy-start.6

commit v2 on v1

--- a/solution.py
+++ b/solution.py
@@ -31,9 +31,9 @@
 
 
 def kernel(
-    q_hbm, k_hbm, v_hbm, res_hbm, wout_hbm, gain_ref, wproj_hbm, texts_ref, labels_ref,
-    hid_hbm, img_ref, txt_ref,
-    q_in, k_in, v_in, res_in, wout, wproj, hid,
+    q_hbm, k_hbm, v_hbm, res_hbm, wout_hbm, gain_hbm, wproj_hbm, texts_hbm, labels_hbm,
+    hid_hbm, losses_ref,
+    q_in, k_in, v_in, res_in, wout, wproj, gain_ref, texts_ref, labels_ref, hid,
     kv_send, q_send, kv_recv, q_recv, o_send, o_recv,
     k_all, vt_all, s_all, acc, t0, tex, e_buf, rows,
     load_sem, kv_ss, kv_rs, q_ss, q_rs, o_ss, o_rs, t0_ss, t0_rs, t1_ss, t1_rs, t2_ss, t2_rs,
@@ -47,11 +47,21 @@
     loads = [
         pltpu.make_async_copy(src, dst, load_sem.at[i])
         for i, (src, dst) in enumerate(
-            [(k_hbm, k_in), (v_hbm, v_in), (q_hbm, q_in), (res_hbm, res_in), (wout_hbm, wout), (wproj_hbm, wproj)]
+            [
+                (k_hbm, k_in),
+                (v_hbm, v_in),
+                (q_hbm, q_in),
+                (res_hbm, res_in),
+                (wout_hbm, wout),
+                (wproj_hbm, wproj),
+                (texts_hbm, texts_ref),
+                (gain_hbm, gain_ref),
+                (labels_hbm, labels_ref),
+            ]
         )
     ]
-    for load in loads[:4]:
-        load.start()
+    for i in (0, 1, 6, 2):
+        loads[i].start()
 
     barrier = pltpu.get_barrier_semaphore()
 
@@ -93,9 +103,10 @@
     turn(k_in, put_k)
     loads[1].wait()
     turn(v_in, put_v)
-    loads[4].start()
-    loads[5].start()
-
+    for i in (3, 4, 5, 7, 8):
+        loads[i].start()
+
+    loads[6].wait()
     piece = texts_ref[...]
     blank = jnp.zeros((1, 64), F32)
     even = jnp.concatenate([piece, blank], axis=1)
@@ -183,8 +194,8 @@
 
         lax.fori_loop(0, NZ, step, 0)
 
+    others(NSEQ, s, lambda p: t0_copy(p, s).start())
     by_depth(1, lambda p: kv_copy(p, s).start())
-    others(NSEQ, s, lambda p: t0_copy(p, s).start())
 
     loads[2].wait()
     turn(q_in, put_q)
@@ -220,6 +231,7 @@
     lax.fori_loop(0, NZ, take_kv, 0)
 
     loads[3].wait()
+    acc[...] = res_in[...].astype(F32)
     factor = HD ** (-0.5) * math.log2(math.e)
 
     def attend(t, c):
@@ -269,8 +281,9 @@
     others(NB2, b_hi, lambda p: t2_copy(p, b_hi).wait_send())
     others(NB2, b_hi, lambda p: t2_copy(b_hi, p).wait_recv())
 
-    acc[...] = res_in[...].astype(F32)
     loads[4].wait()
+    loads[7].wait()
+    loads[8].wait()
 
     def project(t, c):
         there = lax.rem(z + depth_step(t) + NZ, NZ)
@@ -297,10 +310,10 @@
         normed = (centred * lax.rsqrt(variance + 1e-05)).reshape(2, 8, D)
         part = normed[0] + normed[1]
         pool = part if pool is None else pool + part
-    hid_copy = pltpu.make_async_copy(hid, hid_hbm.at[0], load_sem.at[6])
+    hid_copy = pltpu.make_async_copy(hid, hid_hbm.at[0], load_sem.at[9])
     hid_copy.start()
 
-    pooled = jnp.sum(pool, axis=0, keepdims=True) * gain_ref[...] * (1.0 / PATCHES)
+    pooled = jnp.sum(pool, axis=0, keepdims=True) * gain_ref[...].reshape(1, D) * (1.0 / PATCHES)
     first = pooled.astype(BF16).astype(F32)
     rest = pooled - first
     second = rest.astype(BF16).astype(F32)
@@ -314,7 +327,7 @@
     others(NSEQ, s, lambda p: e_copy(p, s).start())
 
     others(NSEQ, s, lambda p: o_copy(p, s).wait_send())
-    label_row = labels_ref[...]
+    label_row = labels_ref[...].reshape(1, NB)
     lane64 = lax.broadcasted_iota(jnp.int32, (1, 64), 1)
     own_label = jnp.sum(jnp.where(lane64 == b, label_row, 0), axis=1, keepdims=True)
     grid_i = lax.broadcasted_iota(jnp.int32, (64, 64), 0)
@@ -335,7 +348,7 @@
     peak = jnp.max(logits, axis=1, keepdims=True)
     lse = peak + jnp.log(jnp.sum(jnp.exp(logits - peak), axis=1, keepdims=True))
     chosen = jnp.sum(jnp.where(lane64 == own_label, logits, 0.0), axis=1, keepdims=True)
-    img_ref[0] = (lse - chosen)[0, 0]
+    image_loss = lse - chosen
     others(NSEQ, s, lambda p: e_copy(p, s).wait_send())
 
     others(NB1, b_lo, lambda p: b1_copy(b_lo, p).wait_recv())
@@ -349,24 +362,21 @@
     high = jnp.max(column, axis=0, keepdims=True)
     total = high + jnp.log(jnp.sum(jnp.exp(column - high), axis=0, keepdims=True))
     match = jnp.sum(jnp.where(label_col == b, column, 0.0), axis=0, keepdims=True)
-    txt_ref[0] = (total - match)[0, 0]
+    losses_ref[...] = jnp.where(lax.broadcasted_iota(jnp.int32, (1, 128), 1) == 0, image_loss, total - match)
     others(NB2, b_hi, lambda p: b2_copy(p, b_hi).wait_send())
 
 
 def body(queries, keys, values, residual_in, w_out, ln_gain, w_proj, texts, labels):
-    any_space = pl.BlockSpec(memory_space=pl.ANY)
-    vmem = pl.BlockSpec(memory_space=pltpu.VMEM)
-    smem = pl.BlockSpec(memory_space=pltpu.SMEM)
+    any_space = pl.BlockSpec(memory_space=pltpu.HBM)
     dma = pltpu.SemaphoreType.DMA
-    out = pl.pallas_call(
+    hidden_out, losses = pl.pallas_call(
         kernel,
         out_shape=(
             jax.ShapeDtypeStruct((1, ROWS, D), BF16),
-            jax.ShapeDtypeStruct((1,), F32),
-            jax.ShapeDtypeStruct((1,), F32),
+            jax.ShapeDtypeStruct((1, 128), F32),
         ),
-        in_specs=[any_space] * 5 + [vmem, any_space, vmem, vmem],
-        out_specs=(any_space, smem, smem),
+        in_specs=[any_space] * 9,
+        out_specs=(any_space, pl.BlockSpec(memory_space=pltpu.VMEM)),
         scratch_shapes=[
             pltpu.VMEM((ROWS, D), BF16),
             pltpu.VMEM((ROWS, D), BF16),
@@ -374,6 +384,9 @@
             pltpu.VMEM((ROWS, D), BF16),
             pltpu.VMEM((D, D), BF16),
             pltpu.VMEM((D, EMBED), BF16),
+            pltpu.VMEM((D,), F32),
+            pltpu.VMEM((1, 64), F32),
+            pltpu.VMEM((NB,), jnp.int32),
             pltpu.VMEM((ROWS, D), BF16),
             pltpu.VMEM((NSEQ, 2 * HD, ROWS), BF16),
             pltpu.VMEM((NSEQ, HD, ROWS), BF16),
@@ -389,7 +402,7 @@
             pltpu.VMEM((NB, 8, 128), F32),
             pltpu.VMEM((NSEQ, 8, 128), F32),
             pltpu.VMEM((NB, 1, 128), F32),
-            dma((8,)),
+            dma((10,)),
             dma((NSEQ,)), dma((NSEQ,)),
             dma((NSEQ,)), dma((NSEQ,)),
             dma((NSEQ,)), dma((NSEQ,)),
@@ -401,7 +414,7 @@
             dma((NB2,)), dma((NB2,)),
         ],
         compiler_params=pltpu.CompilerParams(
-            collective_id=0, has_side_effects=True, vmem_limit_bytes=48 * 1024 * 1024
+            collective_id=0, has_side_effects=True, vmem_limit_bytes=67043328
         ),
         name="attend_and_score",
     )(
@@ -410,12 +423,12 @@
         values.reshape(ROWS, D),
         residual_in.reshape(ROWS, D),
         w_out,
-        ln_gain.reshape(1, D),
+        ln_gain,
         w_proj,
         texts,
-        labels.reshape(1, NB),
+        labels,
     )
-    return out
+    return hidden_out, losses[0, 0:1], losses[0, 1:2]
 
 
 def solution(mesh):

time: 97.2 us -> 82.5 us (0.85)
  Pallas kernels: 84.3 us -> 78.6 us
  local copies, waits for them, and re-layouts: 8.37 us -> 2.99 us
  between operations: 4.14 us -> 0.64 us
    unnamed x15 -> x1, local copies, waits for them, and re-layouts: 7.66 us -> 1.72 us
    pallas_call x1, Pallas kernels: 84.3 us -> 78.6 us  [body(): pl.pallas_call(kernel, out_shape=(jax.ShapeDtypeStruct((1, ROWS, D), BF16...]
    slice x0 -> x1, local copies, waits for them, and re-layouts: none -> 1.27 us  [body(): return (hidden_out, losses[0, 0:1], losses[0, 1:2])]
where the time goes in v2:
time: 82.5 us; the launch traced here: 82.3 us
  Pallas kernels  78.6 us (95%)
  local copies, waits for them, and re-layouts  2.99 us (4%)
    pallas_call x1, Pallas kernels, body(): pl.pallas_call(kernel, out_shape=(jax.ShapeDtypeStruct((1, ROWS, D), BF16...  78.6 us
    unnamed x1, local copies, waits for them, and re-layouts  1.72 us

profile of v2, /device:TPU:1, one launch (start us, length us, event | category | flops | bytes accessed | tf_op | source)
XLA Modules:
  0.0 82.3 jit_solution(17059795900487630668)
XLA Ops:
  0.6 78.6 %attend_and_score.1 = (bf16[1,128,1280]{2,1,0:T(8,128)(2,1)}, f32[1,128]{1,0:T(1,128)}) custom-call(bf16[128,1280]{1,0:T(8,128)(2,1)} %bitcast.6, bf16[128,1280]{1,0:T(8,128)(2,1)} %bitcast.7, bf16[128,1280]{1,0:T(8,128)(2,1)} %bitcast.8, bf16[128,1280]{1,0:T(8,128)(2,1)} %bitcast.9, bf16[1280,1280]{1,0:T(8,128)(2,1)} %wout_hbm.1, f32[1280]{0:T(1024)} %gain_hbm.1, ...), custom_call_target="tpu_custom_call" | custom-call | tf_op jit(solution)/shard_map/attend_and_score/pallas_call | solution.py:372
  79.3 1.3 %fusion = (f32[1,1]{1,0:T(1,128)}, f32[1,1]{1,0:T(1,128)}) fusion(f32[1,128]{1,0:T(1,128)} %get-tuple-element.6), kind=kLoop, calls=%fused_computation | loop fusion | bytes 16 | tf_op jit(solution)/shard_map/slice | solution.py:431
  80.6 1.7 %copy.13 = bf16[1,128,1280]{2,1,0:T(8,128)(2,1)} copy(bf16[1,128,1280]{2,1,0:T(8,128)(2,1)} %get-tuple-element.12) | data formatting | bytes 655360

commit v3 on v2

--- a/solution.py
+++ b/solution.py
@@ -32,8 +32,8 @@
 
 def kernel(
     q_hbm, k_hbm, v_hbm, res_hbm, wout_hbm, gain_hbm, wproj_hbm, texts_hbm, labels_hbm,
-    hid_hbm, losses_ref,
-    q_in, k_in, v_in, res_in, wout, wproj, gain_ref, texts_ref, labels_ref, hid,
+    hid_hbm, losses_hbm,
+    q_in, k_in, v_in, res_in, wout, wproj, gain_ref, texts_ref, labels_ref, hid, losses_ref,
     kv_send, q_send, kv_recv, q_recv, o_send, o_recv,
     k_all, vt_all, s_all, acc, t0, tex, e_buf, rows,
     load_sem, kv_ss, kv_rs, q_ss, q_rs, o_ss, o_rs, t0_ss, t0_rs, t1_ss, t1_rs, t2_ss, t2_rs,
@@ -201,34 +201,31 @@
     turn(q_in, put_q)
     by_depth(1, lambda p: q_copy(p, s).start())
 
+    kv_recv[s] = kv_send[s]
+    q_recv[s] = q_send[s]
+    top = lax.broadcasted_iota(jnp.int32, (16, PATCHES), 0)
+    vt_all[HD : HD + 16, :] = jnp.where(top == 0, 1.0, 0.0).astype(BF16)
+
+    def take_kv(t, c):
+        there = lax.rem(z - depth_step(t) + NZ, NZ)
+        for w in range(2):
+            peer = 2 * there + w
+
+            @pl.when(peer != s)
+            def _():
+                kv_copy(s, peer).wait_recv()
+
+            block = kv_recv[peer]
+            k_all[pl.ds(pl.multiple_of((2 * t + w) * ROWS, ROWS), ROWS), :] = block[:HD].T
+            vt_all[0:HD, pl.ds(pl.multiple_of((2 * t + w) * ROWS, ROWS), ROWS)] = block[HD:]
+        return c
+
+    lax.fori_loop(0, NZ, take_kv, 0)
+
     others(NSEQ, s, lambda p: t0_copy(s, p).wait_recv())
     for k in range(8):
         tex[b, k : k + 1, :] = t0[2 * k] + t0[2 * k + 1]
     others(NB1, b_lo, lambda p: t1_copy(p, b_lo).start())
-
-    kv_recv[s] = kv_send[s]
-    q_recv[s] = q_send[s]
-    top = lax.broadcasted_iota(jnp.int32, (16, PATCHES), 0)
-    vt_all[HD : HD + 16, :] = jnp.where(top == 0, 1.0, 0.0).astype(BF16)
-
-    others(NB1, b_lo, lambda p: t1_copy(b_lo, p).wait_recv())
-    others(NB2, b_hi, lambda p: t2_copy(p, b_hi).start())
-
-    def take_kv(t, c):
-        there = lax.rem(z - depth_step(t) + NZ, NZ)
-        for w in range(2):
-            peer = 2 * there + w
-
-            @pl.when(peer != s)
-            def _():
-                kv_copy(s, peer).wait_recv()
-
-            block = kv_recv[peer]
-            k_all[pl.ds(pl.multiple_of((2 * t + w) * ROWS, ROWS), ROWS), :] = block[:HD].T
-            vt_all[0:HD, pl.ds(pl.multiple_of((2 * t + w) * ROWS, ROWS), ROWS)] = block[HD:]
-        return c
-
-    lax.fori_loop(0, NZ, take_kv, 0)
 
     loads[3].wait()
     acc[...] = res_in[...].astype(F32)
@@ -274,12 +271,12 @@
 
     lax.fori_loop(0, NZ, attend, 0)
 
+    others(NB1, b_lo, lambda p: t1_copy(b_lo, p).wait_recv())
+    others(NB2, b_hi, lambda p: t2_copy(p, b_hi).start())
     others(NSEQ, s, lambda p: kv_copy(p, s).wait_send())
     others(NSEQ, s, lambda p: q_copy(p, s).wait_send())
     others(NSEQ, s, lambda p: t0_copy(p, s).wait_send())
     others(NB1, b_lo, lambda p: t1_copy(p, b_lo).wait_send())
-    others(NB2, b_hi, lambda p: t2_copy(p, b_hi).wait_send())
-    others(NB2, b_hi, lambda p: t2_copy(b_hi, p).wait_recv())
 
     loads[4].wait()
     loads[7].wait()
@@ -336,6 +333,8 @@
         jnp.where(grid_i == grid_j, jnp.broadcast_to(label_row, (64, 64)), 0), axis=1, keepdims=True
     )
 
+    others(NB2, b_hi, lambda p: t2_copy(p, b_hi).wait_send())
+    others(NB2, b_hi, lambda p: t2_copy(b_hi, p).wait_recv())
     others(NSEQ, s, lambda p: e_copy(s, p).wait_recv())
     embedding = jnp.sum(e_buf[...], axis=0)
     squares = jnp.sum(jnp.sum(embedding * embedding, axis=0, keepdims=True), axis=1, keepdims=True)
@@ -363,11 +362,15 @@
     total = high + jnp.log(jnp.sum(jnp.exp(column - high), axis=0, keepdims=True))
     match = jnp.sum(jnp.where(label_col == b, column, 0.0), axis=0, keepdims=True)
     losses_ref[...] = jnp.where(lax.broadcasted_iota(jnp.int32, (1, 128), 1) == 0, image_loss, total - match)
+    losses_copy = pltpu.make_async_copy(losses_ref, losses_hbm, load_sem.at[0])
+    losses_copy.start()
     others(NB2, b_hi, lambda p: b2_copy(p, b_hi).wait_send())
+    losses_copy.wait()
 
 
 def body(queries, keys, values, residual_in, w_out, ln_gain, w_proj, texts, labels):
-    any_space = pl.BlockSpec(memory_space=pltpu.HBM)
+    far_space = pl.BlockSpec(memory_space=pltpu.HBM)
+    any_space = pl.BlockSpec(memory_space=pl.ANY)
     dma = pltpu.SemaphoreType.DMA
     hidden_out, losses = pl.pallas_call(
         kernel,
@@ -375,8 +378,8 @@
             jax.ShapeDtypeStruct((1, ROWS, D), BF16),
             jax.ShapeDtypeStruct((1, 128), F32),
         ),
-        in_specs=[any_space] * 9,
-        out_specs=(any_space, pl.BlockSpec(memory_space=pltpu.VMEM)),
+        in_specs=[far_space] * 9,
+        out_specs=(any_space, any_space),
         scratch_shapes=[
             pltpu.VMEM((ROWS, D), BF16),
             pltpu.VMEM((ROWS, D), BF16),
@@ -388,6 +391,7 @@
             pltpu.VMEM((1, 64), F32),
             pltpu.VMEM((NB,), jnp.int32),
             pltpu.VMEM((ROWS, D), BF16),
+            pltpu.VMEM((1, 128), F32),
             pltpu.VMEM((NSEQ, 2 * HD, ROWS), BF16),
             pltpu.VMEM((NSEQ, HD, ROWS), BF16),
             pltpu.VMEM((NSEQ, 2 * HD, ROWS), BF16),

time: 82.5 us -> 82.7 us (level)
  no operation moved by 1% of the time
where the time goes in v3:
time: 82.7 us; the launch traced here: 82.5 us
  Pallas kernels  78.9 us (95%)
  local copies, waits for them, and re-layouts  2.99 us (4%)
    pallas_call x1, Pallas kernels, body(): pl.pallas_call(kernel, out_shape=(jax.ShapeDtypeStruct((1, ROWS, D), BF16...  78.9 us
    unnamed x1, local copies, waits for them, and re-layouts  1.72 us

profile of v3, /device:TPU:1, one launch (start us, length us, event | category | flops | bytes accessed | tf_op | source)
XLA Modules:
  0.0 82.5 jit_solution(17254333978590231590)
XLA Ops:
  0.6 78.9 %attend_and_score.1 = (bf16[1,128,1280]{2,1,0:T(8,128)(2,1)}, f32[1,128]{1,0:T(1,128)}) custom-call(bf16[128,1280]{1,0:T(8,128)(2,1)} %bitcast.6, bf16[128,1280]{1,0:T(8,128)(2,1)} %bitcast.7, bf16[128,1280]{1,0:T(8,128)(2,1)} %bitcast.8, bf16[128,1280]{1,0:T(8,128)(2,1)} %bitcast.9, bf16[1280,1280]{1,0:T(8,128)(2,1)} %wout_hbm.1, f32[1280]{0:T(1024)} %gain_hbm.1, ...), custom_call_target="tpu_custom_call" | custom-call | tf_op jit(solution)/shard_map/attend_and_score/pallas_call | solution.py:375
  79.5 1.3 %fusion = (f32[1,1]{1,0:T(1,128)}, f32[1,1]{1,0:T(1,128)}) fusion(f32[1,128]{1,0:T(1,128)} %get-tuple-element.6), kind=kLoop, calls=%fused_computation | loop fusion | bytes 16 | tf_op jit(solution)/shard_map/slice | solution.py:435
  80.8 1.7 %copy.13 = bf16[1,128,1280]{2,1,0:T(8,128)(2,1)} copy(bf16[1,128,1280]{2,1,0:T(8,128)(2,1)} %get-tuple-element.12) | data formatting | bytes 655360

commit v4 on v3

--- a/solution.py
+++ b/solution.py
@@ -117,60 +117,67 @@
 
     def kv_copy(to, frm):
         return pltpu.make_async_remote_copy(
-            src_ref=kv_send.at[to], dst_ref=kv_recv.at[frm], send_sem=kv_ss.at[to], recv_sem=kv_rs.at[frm],
+            src_ref=kv_send.at[to], dst_ref=kv_recv.at[frm], send_sem=kv_ss.at[0], recv_sem=kv_rs.at[frm],
             device_id=(b, to), device_id_type=MESH,
         )
 
     def q_copy(to, frm):
         return pltpu.make_async_remote_copy(
-            src_ref=q_send.at[to], dst_ref=q_recv.at[frm], send_sem=q_ss.at[to], recv_sem=q_rs.at[frm],
+            src_ref=q_send.at[to], dst_ref=q_recv.at[frm], send_sem=q_ss.at[0], recv_sem=q_rs.at[frm],
             device_id=(b, to), device_id_type=MESH,
         )
 
     def o_copy(to, frm):
         return pltpu.make_async_remote_copy(
-            src_ref=o_send.at[to], dst_ref=o_recv.at[frm], send_sem=o_ss.at[to], recv_sem=o_rs.at[frm],
+            src_ref=o_send.at[to], dst_ref=o_recv.at[frm], send_sem=o_ss.at[0], recv_sem=o_rs.at[frm],
             device_id=(b, to), device_id_type=MESH,
         )
 
     def t0_copy(to, frm):
         return pltpu.make_async_remote_copy(
-            src_ref=t0.at[frm], dst_ref=t0.at[frm], send_sem=t0_ss.at[to], recv_sem=t0_rs.at[frm],
+            src_ref=t0.at[frm], dst_ref=t0.at[frm], send_sem=t0_ss.at[0], recv_sem=t0_rs.at[0],
             device_id=(b, to), device_id_type=MESH,
         )
 
     def e_copy(to, frm):
         return pltpu.make_async_remote_copy(
-            src_ref=e_buf.at[frm], dst_ref=e_buf.at[frm], send_sem=e_ss.at[to], recv_sem=e_rs.at[frm],
+            src_ref=e_buf.at[frm], dst_ref=e_buf.at[frm], send_sem=e_ss.at[0], recv_sem=e_rs.at[0],
             device_id=(b, to), device_id_type=MESH,
         )
 
     def t1_copy(to, frm):
         at = b_hi * NB1 + frm
         return pltpu.make_async_remote_copy(
-            src_ref=tex.at[at], dst_ref=tex.at[at], send_sem=t1_ss.at[to], recv_sem=t1_rs.at[frm],
+            src_ref=tex.at[at], dst_ref=tex.at[at], send_sem=t1_ss.at[0], recv_sem=t1_rs.at[0],
             device_id=(b_hi * NB1 + to, s), device_id_type=MESH,
         )
 
     def b1_copy(to, frm):
         at = b_hi * NB1 + frm
         return pltpu.make_async_remote_copy(
-            src_ref=rows.at[at], dst_ref=rows.at[at], send_sem=b1_ss.at[to], recv_sem=b1_rs.at[frm],
+            src_ref=rows.at[at], dst_ref=rows.at[at], send_sem=b1_ss.at[0], recv_sem=b1_rs.at[0],
             device_id=(b_hi * NB1 + to, s), device_id_type=MESH,
         )
 
     def t2_copy(to, frm):
         at = pl.ds(frm * NB1, NB1)
         return pltpu.make_async_remote_copy(
-            src_ref=tex.at[at], dst_ref=tex.at[at], send_sem=t2_ss.at[to], recv_sem=t2_rs.at[frm],
+            src_ref=tex.at[at], dst_ref=tex.at[at], send_sem=t2_ss.at[0], recv_sem=t2_rs.at[0],
             device_id=(to * NB1 + b_lo, s), device_id_type=MESH,
         )
 
     def b2_copy(to, frm):
         at = pl.ds(frm * NB1, NB1)
         return pltpu.make_async_remote_copy(
-            src_ref=rows.at[at], dst_ref=rows.at[at], send_sem=b2_ss.at[to], recv_sem=b2_rs.at[frm],
+            src_ref=rows.at[at], dst_ref=rows.at[at], send_sem=b2_ss.at[0], recv_sem=b2_rs.at[0],
             device_id=(to * NB1 + b_lo, s), device_id_type=MESH,
+        )
+
+    def whole(ref, count, send_sem, recv_sem):
+        part = ref.at[pl.ds(0, count)]
+        return pltpu.make_async_remote_copy(
+            src_ref=part, dst_ref=part, send_sem=send_sem.at[0], recv_sem=recv_sem.at[0],
+            device_id=(b, lax.rem(s + 1, NSEQ)), device_id_type=MESH,
         )
 
     def others(count, me, act):
@@ -222,7 +229,7 @@
 
     lax.fori_loop(0, NZ, take_kv, 0)
 
-    others(NSEQ, s, lambda p: t0_copy(s, p).wait_recv())
+    whole(t0, NSEQ - 1, t0_ss, t0_rs).wait_recv()
     for k in range(8):
         tex[b, k : k + 1, :] = t0[2 * k] + t0[2 * k + 1]
     others(NB1, b_lo, lambda p: t1_copy(p, b_lo).start())
@@ -232,6 +239,11 @@
     factor = HD ** (-0.5) * math.log2(math.e)
 
     def attend(t, c):
+        @pl.when(t == 4)
+        def _():
+            whole(tex, NB1 - 1, t1_ss, t1_rs).wait_recv()
+            others(NB2, b_hi, lambda p: t2_copy(p, b_hi).start())
+
         there = lax.rem(z - depth_step(t) + NZ, NZ)
         for w in range(2):
             peer = 2 * there + w
@@ -271,12 +283,10 @@
 
     lax.fori_loop(0, NZ, attend, 0)
 
-    others(NB1, b_lo, lambda p: t1_copy(b_lo, p).wait_recv())
-    others(NB2, b_hi, lambda p: t2_copy(p, b_hi).start())
-    others(NSEQ, s, lambda p: kv_copy(p, s).wait_send())
-    others(NSEQ, s, lambda p: q_copy(p, s).wait_send())
-    others(NSEQ, s, lambda p: t0_copy(p, s).wait_send())
-    others(NB1, b_lo, lambda p: t1_copy(p, b_lo).wait_send())
+    whole(kv_send, NSEQ - 1, kv_ss, kv_rs).wait_send()
+    whole(q_send, NSEQ - 1, q_ss, q_rs).wait_send()
+    whole(t0, NSEQ - 1, t0_ss, t0_rs).wait_send()
+    whole(tex, NB1 - 1, t1_ss, t1_rs).wait_send()
 
     loads[4].wait()
     loads[7].wait()
@@ -323,7 +333,7 @@
         e_buf[s, k : k + 1, :] = projected[:, k * 128 : (k + 1) * 128]
     others(NSEQ, s, lambda p: e_copy(p, s).start())
 
-    others(NSEQ, s, lambda p: o_copy(p, s).wait_send())
+    whole(o_send, NSEQ - 1, o_ss, o_rs).wait_send()
     label_row = labels_ref[...].reshape(1, NB)
     lane64 = lax.broadcasted_iota(jnp.int32, (1, 64), 1)
     own_label = jnp.sum(jnp.where(lane64 == b, label_row, 0), axis=1, keepdims=True)
@@ -333,9 +343,9 @@
         jnp.where(grid_i == grid_j, jnp.broadcast_to(label_row, (64, 64)), 0), axis=1, keepdims=True
     )
 
-    others(NB2, b_hi, lambda p: t2_copy(p, b_hi).wait_send())
-    others(NB2, b_hi, lambda p: t2_copy(b_hi, p).wait_recv())
-    others(NSEQ, s, lambda p: e_copy(s, p).wait_recv())
+    whole(tex, NB - NB1, t2_ss, t2_rs).wait_send()
+    whole(tex, NB - NB1, t2_ss, t2_rs).wait_recv()
+    whole(e_buf, NSEQ - 1, e_ss, e_rs).wait_recv()
     embedding = jnp.sum(e_buf[...], axis=0)
     squares = jnp.sum(jnp.sum(embedding * embedding, axis=0, keepdims=True), axis=1, keepdims=True)
     products = jnp.sum(tex[...] * embedding[None], axis=1)
@@ -348,13 +358,13 @@
     lse = peak + jnp.log(jnp.sum(jnp.exp(logits - peak), axis=1, keepdims=True))
     chosen = jnp.sum(jnp.where(lane64 == own_label, logits, 0.0), axis=1, keepdims=True)
     image_loss = lse - chosen
-    others(NSEQ, s, lambda p: e_copy(p, s).wait_send())
-
-    others(NB1, b_lo, lambda p: b1_copy(b_lo, p).wait_recv())
+    whole(e_buf, NSEQ - 1, e_ss, e_rs).wait_send()
+
+    whole(rows, NB1 - 1, b1_ss, b1_rs).wait_recv()
     others(NB2, b_hi, lambda p: b2_copy(p, b_hi).start())
-    others(NB1, b_lo, lambda p: b1_copy(p, b_lo).wait_send())
+    whole(rows, NB1 - 1, b1_ss, b1_rs).wait_send()
     hid_copy.wait()
-    others(NB2, b_hi, lambda p: b2_copy(b_hi, p).wait_recv())
+    whole(rows, NB - NB1, b2_ss, b2_rs).wait_recv()
 
     lane128 = lax.broadcasted_iota(jnp.int32, (64, 128), 1)
     column = jnp.sum(jnp.where(lane128 == b, rows[...].reshape(64, 128), 0.0), axis=1, keepdims=True)
@@ -364,8 +374,27 @@
     losses_ref[...] = jnp.where(lax.broadcasted_iota(jnp.int32, (1, 128), 1) == 0, image_loss, total - match)
     losses_copy = pltpu.make_async_copy(losses_ref, losses_hbm, load_sem.at[0])
     losses_copy.start()
-    others(NB2, b_hi, lambda p: b2_copy(p, b_hi).wait_send())
+    whole(rows, NB - NB1, b2_ss, b2_rs).wait_send()
     losses_copy.wait()
+
+
+def hand_over(hid_hbm, losses_hbm, out_hbm, img_ref, txt_ref, held, scores, in_sem, out_sem):
+    quarter = ROWS // 4
+    cuts = [pl.ds(i * quarter, quarter) for i in range(4)]
+    read = [pltpu.make_async_copy(hid_hbm.at[0, cut], held.at[cut], in_sem.at[i]) for i, cut in enumerate(cuts)]
+    write = [pltpu.make_async_copy(held.at[cut], out_hbm.at[0, cut], out_sem.at[i]) for i, cut in enumerate(cuts)]
+    numbers = pltpu.make_async_copy(losses_hbm, scores, in_sem.at[4])
+    numbers.start()
+    for r in read:
+        r.start()
+    for r, w in zip(read, write):
+        r.wait()
+        w.start()
+    numbers.wait()
+    img_ref[0] = scores[0, 0]
+    txt_ref[0] = scores[0, 1]
+    for w in write:
+        w.wait()
 
 
 def body(queries, keys, values, residual_in, w_out, ln_gain, w_proj, texts, labels):
@@ -407,15 +436,15 @@
             pltpu.VMEM((NSEQ, 8, 128), F32),
             pltpu.VMEM((NB, 1, 128), F32),
             dma((10,)),
-            dma((NSEQ,)), dma((NSEQ,)),
-            dma((NSEQ,)), dma((NSEQ,)),
-            dma((NSEQ,)), dma((NSEQ,)),
-            dma((NSEQ,)), dma((NSEQ,)),
-            dma((NB1,)), dma((NB1,)),
-            dma((NB2,)), dma((NB2,)),
-            dma((NSEQ,)), dma((NSEQ,)),
-            dma((NB1,)), dma((NB1,)),
-            dma((NB2,)), dma((NB2,)),
+            dma((1,)), dma((NSEQ,)),
+            dma((1,)), dma((NSEQ,)),
+            dma((1,)), dma((NSEQ,)),
+            dma((1,)), dma((1,)),
+            dma((1,)), dma((1,)),
+            dma((1,)), dma((1,)),
+            dma((1,)), dma((1,)),
+            dma((1,)), dma((1,)),
+            dma((1,)), dma((1,)),
         ],
         compiler_params=pltpu.CompilerParams(
             collective_id=0, has_side_effects=True, vmem_limit_bytes=67043328
@@ -432,7 +461,20 @@
         texts,
         labels,
     )
-    return hidden_out, losses[0, 0:1], losses[0, 1:2]
+    smem = pl.BlockSpec(memory_space=pltpu.SMEM)
+    return pl.pallas_call(
+        hand_over,
+        out_shape=(
+            jax.ShapeDtypeStruct((1, ROWS, D), BF16),
+            jax.ShapeDtypeStruct((1,), F32),
+            jax.ShapeDtypeStruct((1,), F32),
+        ),
+        in_specs=[any_space] * 2,
+        out_specs=(any_space, smem, smem),
+        scratch_shapes=[pltpu.VMEM((ROWS, D), BF16), pltpu.SMEM((1, 128), F32), dma((5,)), dma((4,))],
+        compiler_params=pltpu.CompilerParams(vmem_limit_bytes=67043328),
+        name="hand_over",
+    )(hidden_out, losses)
 
 
 def solution(mesh):

time: 82.7 us -> 80.9 us (0.978)
  local copies, waits for them, and re-layouts: 2.99 us -> 0 us
  Pallas kernels: 78.9 us -> 80 us
    pallas_call x0 -> x1, Pallas kernels: none -> 2.25 us  [body(): pl.pallas_call(hand_over, out_shape=(jax.ShapeDtypeStruct((1, ROWS, D), B...]
    unnamed x1 -> x0, local copies, waits for them, and re-layouts: 1.72 us -> none
    slice x1 -> x0, local copies, waits for them, and re-layouts: 1.27 us -> none  [body(): return (hidden_out, losses[0, 0:1], losses[0, 1:2])]
    pallas_call x1, Pallas kernels: 78.9 us -> 77.8 us  [body(): pl.pallas_call(kernel, out_shape=(jax.ShapeDtypeStruct((1, ROWS, D), BF16...]
where the time goes in v4:
time: 80.9 us; the launch traced here: 80.7 us
  Pallas kernels  80 us (99%)
    pallas_call x1, Pallas kernels, body(): pl.pallas_call(kernel, out_shape=(jax.ShapeDtypeStruct((1, ROWS, D), BF16...  77.8 us
    pallas_call x1, Pallas kernels, body(): pl.pallas_call(hand_over, out_shape=(jax.ShapeDtypeStruct((1, ROWS, D), B...  2.25 us

profile of v4, /device:TPU:1, one launch (start us, length us, event | category | flops | bytes accessed | tf_op | source)
XLA Modules:
  0.0 80.7 jit_solution(1754901640961494524)
XLA Ops:
  0.6 77.8 %attend_and_score.1 = (bf16[1,128,1280]{2,1,0:T(8,128)(2,1)}, f32[1,128]{1,0:T(1,128)}) custom-call(bf16[128,1280]{1,0:T(8,128)(2,1)} %bitcast.4, bf16[128,1280]{1,0:T(8,128)(2,1)} %bitcast.5, bf16[128,1280]{1,0:T(8,128)(2,1)} %bitcast.6, bf16[128,1280]{1,0:T(8,128)(2,1)} %bitcast.7, bf16[1280,1280]{1,0:T(8,128)(2,1)} %wout_hbm.1, f32[1280]{0:T(1024)} %gain_hbm.1, ...), custom_call_target="tpu_custom_call" | custom-call | tf_op jit(solution)/shard_map/attend_and_score/pallas_call | solution.py:404
  78.4 2.2 %hand_over.1 = (bf16[1,128,1280]{2,1,0:T(8,128)(2,1)}, f32[1]{0:T(128)}, f32[1]{0:T(128)}) custom-call(bf16[1,128,1280]{2,1,0:T(8,128)(2,1)} %get-tuple-element.5.hid_hbm, f32[1,128]{1,0:T(1,128)} %get-tuple-element.6.losses_hbm), custom_call_target="tpu_custom_call" | custom-call | tf_op jit(solution)/shard_map/hand_over/pallas_call | solution.py:465

commit v5 on v4

--- a/solution.py
+++ b/solution.py
@@ -189,7 +189,7 @@
 
     def by_depth(sign, act):
         def step(t, c):
-            there = lax.rem(z + sign * depth_step(t) + NZ, NZ)
+            there = lax.rem(z + sign * depth_step(NZ - 1 - t) + NZ, NZ)
             for w in range(2):
                 peer = 2 * there + lax.rem(y + w, 2)
 
@@ -214,7 +214,7 @@
     vt_all[HD : HD + 16, :] = jnp.where(top == 0, 1.0, 0.0).astype(BF16)
 
     def take_kv(t, c):
-        there = lax.rem(z - depth_step(t) + NZ, NZ)
+        there = lax.rem(z - depth_step(NZ - 1 - t) + NZ, NZ)
         for w in range(2):
             peer = 2 * there + w
 
@@ -239,49 +239,55 @@
     factor = HD ** (-0.5) * math.log2(math.e)
 
     def attend(t, c):
-        @pl.when(t == 4)
+        @pl.when(t == 2)
         def _():
             whole(tex, NB1 - 1, t1_ss, t1_rs).wait_recv()
             others(NB2, b_hi, lambda p: t2_copy(p, b_hi).start())
 
-        there = lax.rem(z - depth_step(t) + NZ, NZ)
-        for w in range(2):
-            peer = 2 * there + w
-
-            @pl.when(peer != s)
-            def _():
-                q_copy(s, peer).wait_recv()
-
-        qt = jnp.concatenate([q_recv[2 * there], q_recv[2 * there + 1]], axis=1)
-        top8 = None
-        for i in range(PATCHES // KB):
-            part = jnp.dot(k_all[i * KB : (i + 1) * KB, :], qt, preferred_element_type=F32)
-            s_all[i * KB : (i + 1) * KB, :] = part
-            high = jnp.max(part.reshape(KB // 8, 8, CHUNK), axis=0)
-            top8 = high if top8 is None else jnp.maximum(top8, high)
-        maxima = jnp.max(top8, axis=0, keepdims=True)
-        total = None
-        for i in range(PATCHES // KB):
-            weights = jnp.exp2((s_all[i * KB : (i + 1) * KB, :] - maxima) * factor).astype(BF16)
-            part = jnp.dot(vt_all[:, i * KB : (i + 1) * KB], weights, preferred_element_type=F32)
-            total = part if total is None else total + part
-        mixed = (total[:HD] / total[HD : HD + 1]).astype(BF16)
-        for w in range(2):
-            peer = 2 * there + w
-            value = mixed[:, w * ROWS : (w + 1) * ROWS]
-
-            @pl.when(peer != s)
-            def _():
-                o_send[peer] = value
-                o_copy(peer, s).start()
-
-            @pl.when(peer == s)
-            def _():
-                o_recv[s] = value
+        depths = [lax.rem(z - depth_step(2 * t + u) + NZ, NZ) for u in range(2)]
+        for there in depths:
+            for w in range(2):
+                peer = 2 * there + w
+
+                @pl.when(peer != s)
+                def _():
+                    q_copy(s, peer).wait_recv()
+
+        maxima = []
+        for u, there in enumerate(depths):
+            qt = jnp.concatenate([q_recv[2 * there], q_recv[2 * there + 1]], axis=1)
+            top8 = None
+            for i in range(PATCHES // KB):
+                part = jnp.dot(k_all[i * KB : (i + 1) * KB, :], qt, preferred_element_type=F32)
+                s_all[u, i * KB : (i + 1) * KB, :] = part
+                high = jnp.max(part.reshape(KB // 8, 8, CHUNK), axis=0)
+                top8 = high if top8 is None else jnp.maximum(top8, high)
+            maxima.append(jnp.max(top8, axis=0, keepdims=True))
+        mixed = []
+        for u in range(2):
+            total = None
+            for i in range(PATCHES // KB):
+                weights = jnp.exp2((s_all[u, i * KB : (i + 1) * KB, :] - maxima[u]) * factor).astype(BF16)
+                part = jnp.dot(vt_all[:, i * KB : (i + 1) * KB], weights, preferred_element_type=F32)
+                total = part if total is None else total + part
+            mixed.append((total[:HD] / total[HD : HD + 1]).astype(BF16))
+        for u, there in enumerate(depths):
+            for w in range(2):
+                peer = 2 * there + w
+                value = mixed[u][:, w * ROWS : (w + 1) * ROWS]
+
+                @pl.when(peer != s)
+                def _():
+                    o_send[peer] = value
+                    o_copy(peer, s).start()
+
+                @pl.when(peer == s)
+                def _():
+                    o_recv[s] = value
 
         return c
 
-    lax.fori_loop(0, NZ, attend, 0)
+    lax.fori_loop(0, NZ // 2, attend, 0)
 
     whole(kv_send, NSEQ - 1, kv_ss, kv_rs).wait_send()
     whole(q_send, NSEQ - 1, q_ss, q_rs).wait_send()
@@ -429,7 +435,7 @@
             pltpu.VMEM((NSEQ, HD, ROWS), BF16),
             pltpu.VMEM((PATCHES, HD), BF16),
             pltpu.VMEM((HD + 16, PATCHES), BF16),
-            pltpu.VMEM((PATCHES, CHUNK), F32),
+            pltpu.VMEM((2, PATCHES, CHUNK), F32),
             pltpu.VMEM((ROWS, D), F32),
             pltpu.VMEM((NSEQ, 1, 128), F32),
             pltpu.VMEM((NB, 8, 128), F32),

time: 80.9 us -> 82.1 us (1.015)
  Pallas kernels: 80 us -> 81.2 us
    pallas_call x1, Pallas kernels: 77.8 us -> 79 us  [body(): pl.pallas_call(kernel, out_shape=(jax.ShapeDtypeStruct((1, ROWS, D), BF16...]
where the time goes in v5:
time: 82.1 us; the launch traced here: 81.8 us
  Pallas kernels  81.2 us (99%)
    pallas_call x1, Pallas kernels, body(): pl.pallas_call(kernel, out_shape=(jax.ShapeDtypeStruct((1, ROWS, D), BF16...  79 us
    pallas_call x1, Pallas kernels, body(): pl.pallas_call(hand_over, out_shape=(jax.ShapeDtypeStruct((1, ROWS, D), B...  2.25 us

profile of v5, /device:TPU:1, one launch (start us, length us, event | category | flops | bytes accessed | tf_op | source)
XLA Modules:
  0.0 81.8 jit_solution(6006205284199533700)
XLA Ops:
  0.6 79.0 %attend_and_score.1 = (bf16[1,128,1280]{2,1,0:T(8,128)(2,1)}, f32[1,128]{1,0:T(1,128)}) custom-call(bf16[128,1280]{1,0:T(8,128)(2,1)} %bitcast.4, bf16[128,1280]{1,0:T(8,128)(2,1)} %bitcast.5, bf16[128,1280]{1,0:T(8,128)(2,1)} %bitcast.6, bf16[128,1280]{1,0:T(8,128)(2,1)} %bitcast.7, bf16[1280,1280]{1,0:T(8,128)(2,1)} %wout_hbm.1, f32[1280]{0:T(1024)} %gain_hbm.1, ...), custom_call_target="tpu_custom_call" | custom-call | tf_op jit(solution)/shard_map/attend_and_score/pallas_call | solution.py:410
  79.6 2.2 %hand_over.1 = (bf16[1,128,1280]{2,1,0:T(8,128)(2,1)}, f32[1]{0:T(128)}, f32[1]{0:T(128)}) custom-call(bf16[1,128,1280]{2,1,0:T(8,128)(2,1)} %get-tuple-element.5.hid_hbm, f32[1,128]{1,0:T(1,128)} %get-tuple-element.6.losses_hbm), custom_call_target="tpu_custom_call" | custom-call | tf_op jit(solution)/shard_map/hand_over/pallas_call | solution.py:471
